TPU v7x, 256 devices: a whole 4x4x8 slice. The times are simulated.
256 devices in a mesh: dp: 2 (over core), seq: 32 (over z, x), mp: 4 (over y).
Axes of the slice: x: 4, y: 4, z: 8, core: 2. Of those that a mesh axis runs over, the one named last changes fastest.
Arguments:
- queries: bfloat16 [6, 4096, 4096], P('dp', 'seq', 'mp'), may hold values from -1000 to 1000
- database: bfloat16 [1024, 128, 1024], P('seq', None, 'mp'), may hold values from -300 to 300
- owner_ids: int32 [2, 32, 6, 2], P('dp'), may hold values from 0 to 31, all different within a row; in each aligned block of 6 rows (0 to 5, 6 to 11, ..., all dimensions but the last counted through in order) at most 2 rows name the same one
- row_ids: int32 [2, 32, 6, 2], P('dp'), may hold values from 0 to 31
- pre_gain: float32 [1024], replicated, may hold values from 0.1 to 1.9
- out_gain: float32 [1024], replicated, may hold values from 0.1 to 1.9
- w_in: bfloat16 [1024, 4096], P(None, 'mp'), may hold values from -0.1875 to 0.1875
- w_out: bfloat16 [4096, 1024], P('mp'), may hold values from -0.09375 to 0.09375
- w_key: bfloat16 [1024, 4096], P(None, 'mp'), may hold values from -0.1875 to 0.1875
- w_value: bfloat16 [1024, 4096], P(None, 'mp'), may hold values from -0.1875 to 0.1875
Outputs:
- attended: bfloat16 [6, 4096, 4096], P('dp', 'seq', 'mp')
Inputs may be any that keep to these rules, and one draw needn't show every extreme that they name: `owner_ids`: within one index pair of the first two dimensions (the 6 spans of one device) no shard number appears more than 2 times, and the 2 neighbours of one span lie on different shards.
All inputs are finite; a program needn't handle non-finite values.
Results may differ from a plain program's by a relative error of at most 0.04.
Values may be sent and summed in bfloat16 or wider, within the bound.
No kernel may reach another device: no remote copies, remote signals or barrier semaphores. Data moves between devices by JAX's collectives and lax.ppermute only.
A program may use at most 64 MiB of HBM per device.

v0:
```python
import jax
import jax.numpy as jnp
from jax import lax
from jax.sharding import PartitionSpec as P

HD = 128
MOST = 2
epsilon = 1e-06


def passed_along(array, axis, by):
    peers = lax.axis_size(axis)
    pairs = [(i, i + by) for i in range(peers) if 0 <= i + by < peers]
    return lax.ppermute(array, axis, pairs)


def rms_scale(values, gain_values):
    return (
        values
        * lax.rsqrt(jnp.mean(values * values, axis=-1, keepdims=True) + epsilon)
        * gain_values
    )


def body(queries, database, owner_ids, row_ids, pre_gain, out_gain, w_in, w_out, w_key, w_value):
    shards = lax.axis_size("seq")
    my_index = lax.axis_index("seq")
    seq_count, length, local_width = queries.shape
    slot_count = owner_ids.shape[2]
    per_span = slot_count // seq_count
    neigh_count = owner_ids.shape[3]
    block_len = database.shape[1]
    requests = slot_count * neigh_count
    owners = owner_ids[0].reshape(shards, requests)
    row_index = row_ids[0].reshape(shards, requests)
    position = jnp.arange(requests)
    before = position[None, :] < position[:, None]
    slot_rank = jnp.sum((owners[:, :, None] == owners[:, None, :]) & before[None], axis=2)
    own_owner = lax.dynamic_index_in_dim(owners, my_index, 0, keepdims=False)
    own_rank = lax.dynamic_index_in_dim(slot_rank, my_index, 0, keepdims=False)
    is_mine = (owners == my_index)[:, None, :] & (
        slot_rank[:, None, :] == jnp.arange(MOST)[:, None]
    )
    wanted = jnp.sum(jnp.where(is_mine, row_index[:, None, :], 0), axis=2)
    sending = jnp.take(database, wanted.reshape(-1), axis=0)
    arrived = lax.all_to_all(
        sending.reshape((shards, MOST) + database.shape[1:]),
        "seq",
        split_axis=0,
        concat_axis=0,
        tiled=True,
    )
    stacked = arrived.reshape((shards * MOST,) + arrived.shape[2:])
    blocks = jnp.take(stacked, own_owner * MOST + own_rank, axis=0)
    blocks = blocks.reshape((seq_count, per_span, neigh_count, block_len, blocks.shape[-1]))
    arrived_rows = passed_along(blocks[:, -1], "seq", 1)
    blocks = jnp.concatenate([arrived_rows[:, None], blocks[:, :-1]], axis=1)
    blocks = lax.all_gather(blocks, "mp", axis=4, tiled=True)
    features = blocks.shape[-1]
    widened = blocks.reshape(-1, features).astype(jnp.float32)
    normed = rms_scale(widened, pre_gain).astype(jnp.bfloat16)
    hidden_act = jax.nn.gelu(jnp.dot(normed, w_in, preferred_element_type=jnp.float32)).astype(
        jnp.bfloat16
    )
    summed = lax.psum(
        jnp.dot(hidden_act, w_out, preferred_element_type=jnp.float32).astype(jnp.bfloat16), "mp"
    ).astype(jnp.float32)
    encoded = rms_scale(widened + summed, out_gain).astype(jnp.bfloat16)
    key_rows = jnp.dot(encoded, w_key, preferred_element_type=jnp.float32).astype(jnp.bfloat16)
    value_rows = jnp.dot(encoded, w_value, preferred_element_type=jnp.float32).astype(jnp.bfloat16)
    key_rows = key_rows.reshape(seq_count, per_span, neigh_count * block_len, local_width)
    value_rows = value_rows.reshape(seq_count, per_span, neigh_count * block_len, local_width)
    head_count = local_width // HD
    span_len = length // per_span
    query_rows = queries.reshape(seq_count, per_span, span_len, head_count, HD)
    key_rows = key_rows.reshape(seq_count, per_span, neigh_count * block_len, head_count, HD)
    value_rows = value_rows.reshape(seq_count, per_span, neigh_count * block_len, head_count, HD)
    scores = jnp.einsum(
        "scqhd,sckhd->schqk", query_rows, key_rows, preferred_element_type=jnp.float32
    ) * HD ** (-0.5)
    scores = scores - jnp.max(scores, axis=-1, keepdims=True)
    weights = jnp.exp(scores)
    weights = (weights / jnp.sum(weights, axis=-1, keepdims=True)).astype(jnp.bfloat16)
    attended = jnp.einsum(
        "schqk,sckhd->scqhd", weights, value_rows, preferred_element_type=jnp.float32
    )
    has_source = my_index * per_span + jnp.arange(per_span) > 0
    attended = jnp.where(has_source[None, :, None, None, None], attended, 0.0)
    return attended.astype(jnp.bfloat16).reshape(seq_count, length, local_width)


def solution(mesh):
    return jax.shard_map(
        body,
        mesh=mesh,
        in_specs=(
            P("dp", "seq", "mp"),
            P("seq", None, "mp"),
            P("dp", None, None, None),
            P("dp", None, None, None),
            P(),
            P(),
            P(None, "mp"),
            P("mp", None),
            P(None, "mp"),
            P(None, "mp"),
        ),
        out_specs=P("dp", "seq", "mp"),
        check_vma=False,
    )
```

profile of v0, /device:TPU:1, one launch (start us, length us, event | category | flops | bytes accessed | tf_op | source)
XLA Modules:
  0.0 324.7 jit_solution(9118255975437345221)
XLA Ops:
  6.5 0.8 reshape_squeeze.3
  7.5 0.7 broadcast_in_dim.63
  8.6 2.8 gather_fusion
  11.4 4.5 %broadcast_select_fusion = bf16[32,2,128,256]{3,2,1,0:T(8,128)(2,1)} fusion(bf16[32,2,128,256]{3,2,1,0:T(8,128)(2,1)} %bitcast.73, pred[32,2]{1,0:T(8,128)(4,1)S(1)} %copy.37), kind=kLoop, calls=%fused_computation.20 | loop fusion | flops 2097152 | bytes 8388672 | tf_op jit(solution)/shard_map/jit(_take)/select_n | solution.py:45
  15.9 12.0 %all-to-all-start = ((bf16[32,2,128,256]{3,2,1,0:T(8,128)(2,1)}), bf16[32,2,128,256]{3,2,1,0:T(8,128)(2,1)}, u32[]{:S(2)}, u32[]{:S(2)}) async-start(bf16[32,2,128,256]{3,2,1,0:T(8,128)(2,1)} %broadcast_select_fusion), calls=%async_computation | async-start | bytes 8388608 | tf_op jit(solution)/shard_map/all_to_all | solution.py:46
  28.0 0.2 add_reduce_fusion
  28.3 92.7 %all-to-all-done = bf16[32,2,128,256]{3,2,1,0:T(8,128)(2,1)} async-done(((bf16[32,2,128,256]{3,2,1,0:T(8,128)(2,1)}), bf16[32,2,128,256]{3,2,1,0:T(8,128)(2,1)}, u32[]{:S(2)}, u32[]{:S(2)}) %all-to-all-start) | async-done | bytes 4194336 | tf_op jit(solution)/shard_map/all_to_all | solution.py:46
  121.0 2.8 gather_fusion.1
  123.7 0.1 broadcast_select_fusion.1
  124.0 4.6 %collective-permute-start = (bf16[3,2,128,256]{3,2,1,0:T(8,128)(2,1)S(1)}, bf16[3,2,128,256]{3,2,1,0:T(8,128)(2,1)S(1)}, u32[]{:S(2)}, u32[]{:S(2)}) collective-permute-start(bf16[3,2,128,256]{3,2,1,0:T(8,128)(2,1)S(1)} %get-tuple-element.5), channel_id=1, source_target_pairs={{0,4},{4,8},{8,12},{12,16},{16,20},{20,24},{24,28},{28,32},{32,36}... | collective-permute-start | bytes 1179656 | tf_op jit(solution)/shard_map/ppermute | solution.py:14
  128.6 5.2 %collective-permute-done = bf16[3,2,128,256]{3,2,1,0:T(8,128)(2,1)S(1)} collective-permute-done((bf16[3,2,128,256]{3,2,1,0:T(8,128)(2,1)S(1)}, bf16[3,2,128,256]{3,2,1,0:T(8,128)(2,1)S(1)}, u32[]{:S(2)}, u32[]{:S(2)}) %collective-permute-start) | collective-permute-done | bytes 393248 | tf_op jit(solution)/shard_map/ppermute | solution.py:14
  133.7 0.9 pad_maximum_fusion
  134.8 47.7 %all-gather.2.cloned.1.call-done = bf16[3,2,2,128,1024]{4,3,2,1,0:T(8,128)(2,1)} async-done(((bf16[3,2,2,128,256]{4,3,2,1,0:T(8,128)(2,1)}), bf16[3,2,2,128,1024]{4,3,2,1,0:T(8,128)(2,1)}) %all-gather.2.cloned.1.call-update) | async-done | bytes 3145744 | tf_op jit(solution)/shard_map/all_gather | solution.py:58
  182.5 2.6 fusion.9
  185.1 4.4 %fusion.11 = bf16[1536,1024]{1,0:T(8,128)(2,1)} fusion(bf16[3,2,2,128,1024]{4,3,2,1,0:T(8,128)(2,1)} %all-gather.2.cloned.1.call-done, f32[1024]{0:T(1024)S(1)} %copy-done.5, f32[1536]{0:T(1024)S(1)} %rsqrt.20), kind=kLoop, calls=%fused_computation.17 | loop fusion | flops 6291456 | bytes 6301696 | tf_op jit(solution)/shard_map/convert_element_type | solution.py:61
  189.5 10.9 %convolution_convert_fusion.2 = bf16[1536,1024]{1,0:T(8,128)(2,1)} fusion(bf16[1024,1024]{1,0:T(8,128)(2,1)} %param.17, bf16[1536,1024]{1,0:T(8,128)(2,1)} %fusion.11, bf16[1024,1024]{1,0:T(8,128)(2,1)} %param.16), kind=kOutput, calls=%fused_computation.23 | convolution fusion | flops 6458179584 | bytes 10485760 | tf_op jit(solution)/shard_map/dot_general | solution.py:66
  200.4 1.3 copy.46
  201.8 81.8 %all-reduce.2.cloned.1.call-done = bf16[1536,1024]{1,0:T(8,128)(2,1)} async-done(((bf16[1536,1024]{1,0:T(8,128)(2,1)}), bf16[1536,1024]{1,0:T(8,128)(2,1)}) %all-reduce.2.cloned.1.call-update) | async-done | bytes 3145744 | tf_op jit(solution)/shard_map/psum | solution.py:65
  283.6 4.1 %multiply_reduce_fusion = f32[1536]{0:T(1024)S(1)} fusion(bf16[1536,1024]{1,0:T(8,128)(2,1)} %all-reduce.2.cloned.1.call-done, bf16[3,2,2,128,1024]{4,3,2,1,0:T(8,128)(2,1)} %all-gather.2.cloned.1.call-done), kind=kLoop, calls=%fused_computation.19 | loop fusion | flops 7862784 | bytes 6297600 | tf_op jit(solution)/shard_map/reduce_sum | solution.py:20
  287.7 0.6 copy-done.2
  288.3 1.1 multiply_convert_fusion
  289.4 0.4 copy-done.6
  289.9 3.6 %fusion.27 = bf16[192,8,8,128]{3,1,2,0:T(8,128)(2,1)S(1)} fusion(bf16[1536,1024]{1,0:T(8,128)(2,1)S(1)} %multiply_convert_fusion, bf16[1024,1024]{1,0:T(8,128)(2,1)S(1)} %copy-done.6), kind=kOutput, calls=%fused_computation.39 | convolution fusion | flops 3222798336 | bytes 8388608 | tf_op jit(solution)/shard_map/dot_general | solution.py:69
  293.5 0.8 copy.45
  294.3 1.2 fusion.17
  295.6 1.1 fusion.51
  296.7 1.6 copy-done.7
  298.3 3.9 %fusion.26 = bf16[192,8,8,128]{3,1,2,0:T(8,128)(2,1)S(1)} fusion(bf16[1536,1024]{1,0:T(8,128)(2,1)S(1)} %multiply_convert_fusion, bf16[1024,1024]{1,0:T(8,128)(2,1)S(1)} %copy-done.7), kind=kOutput, calls=%fused_computation.38 | convolution fusion | flops 3222798336 | bytes 8388608 | tf_op jit(solution)/shard_map/dot_general | solution.py:70
  302.1 2.5 copy.47
  304.6 10.3 %fusion.32 = bf16[3,2,64,8,128]{4,2,3,1,0:T(8,128)(2,1)} fusion(bf16[3,2,256,8,128]{4,3,2,1,0:T(8,128)(2,1)} %bitcast.76, f32[3,2,8,64]{3,2,1,0:T(8,128)S(1)} %fusion.51, pred[2]{0:T(512)(128)(4,1)S(1)} %add_compare_fusion, f32[3,2,8,256,64]{3,4,2,1,0:T(8,128)} %copy-done.3), kind=kOutput, calls=%fused_computation.43 | convolution fusion | flops 206048512 | bytes 7090178 | tf_op jit(solution)/shard_map/schqk,sckhd->scqhd/dot_general | solution.py:84
  315.0 1.7 copy.43
  316.6 1.2 reshape.158
  (36 shorter events, 0.8 us)
Async XLA Ops:
  6.5 2.0 copy-start
  15.9 105.0 %all-to-all-start = ((bf16[32,2,128,256]{3,2,1,0:T(8,128)(2,1)}), bf16[32,2,128,256]{3,2,1,0:T(8,128)(2,1)}, u32[]{:S(2)}, u32[]{:S(2)}) async-start(bf16[32,2,128,256]{3,2,1,0:T(8,128)(2,1)} %broadcast_select_fusion), calls=%async_computation | async-start | bytes 8388608 | tf_op jit(solution)/shard_map/all_to_all | solution.py:46
  27.9 154.6 %all-gather.2.cloned.1.call-start = ((), (), s32[]{:S(2)}) async-start(), calls=%async_computation.1 | async-start | bytes 3932160 | tf_op jit(solution)/shard_map/all_gather | solution.py:58
  124.0 61.1 %copy-start.5 = (f32[1024]{0:T(1024)S(1)}, f32[1024]{0:T(1024)}, u32[]{:S(2)}) copy-start(f32[1024]{0:T(1024)} %param.14) | copy-start | bytes 12292
  124.0 9.8 %collective-permute-start = (bf16[3,2,128,256]{3,2,1,0:T(8,128)(2,1)S(1)}, bf16[3,2,128,256]{3,2,1,0:T(8,128)(2,1)S(1)}, u32[]{:S(2)}, u32[]{:S(2)}) collective-permute-start(bf16[3,2,128,256]{3,2,1,0:T(8,128)(2,1)S(1)} %get-tuple-element.5), channel_id=1, source_target_pairs={{0,4},{4,8},{8,12},{12,16},{16,20},{20,24},{24,28},{28,32},{32,36}... | collective-permute-start | bytes 1179656 | tf_op jit(solution)/shard_map/ppermute | solution.py:14
  134.7 148.9 %all-reduce.2.cloned.1.call-start = ((), (), s32[]{:S(2)}) async-start(), calls=%async_computation.2 | async-start | bytes 6291456 | tf_op jit(solution)/shard_map/psum | solution.py:65
  201.7 85.9 %copy-start.4 = (f32[1024]{0:T(1024)S(1)}, f32[1024]{0:T(1024)}, u32[]{:S(2)}) copy-start(f32[1024]{0:T(1024)} %param.15) | copy-start | bytes 12292
  283.6 4.1 %copy-start.1 = (bf16[3,2,2,128,1024]{4,3,2,1,0:T(8,128)(2,1)S(1)}, bf16[3,2,2,128,1024]{4,3,2,1,0:T(8,128)(2,1)}, u32[]{:S(2)}) copy-start(bf16[3,2,2,128,1024]{4,3,2,1,0:T(8,128)(2,1)} %all-gather.2.cloned.1.call-done) | copy-start | bytes 9437188
  283.6 4.7 %copy-start.2 = (bf16[1536,1024]{1,0:T(8,128)(2,1)S(1)}, bf16[1536,1024]{1,0:T(8,128)(2,1)}, u32[]{:S(2)}) copy-start(bf16[1536,1024]{1,0:T(8,128)(2,1)} %all-reduce.2.cloned.1.call-done) | copy-start | bytes 9437188
  288.3 1.6 copy-start.6
  295.5 6.6 %copy-start.3 = (f32[3,2,8,256,64]{3,4,2,1,0:T(8,128)}, f32[3,2,8,256,64]{3,4,2,1,0:T(8,128)S(1)}, u32[]{:S(2)}) copy-start(f32[3,2,8,256,64]{3,4,2,1,0:T(8,128)S(1)} %fusion.17) | copy-start | bytes 9437188
  295.5 2.7 copy-start.7
Sparse Core Ops, SparseCore 0:
  134.8 47.5 all-gather.1
  200.5 82.9 all-reduce.1
where the time goes:
time: 325 us
  waiting for transfers between devices  227 us (70%)
  matrix products  29.9 us (9%)
  other arithmetic  19.3 us (6%)
  local copies, waits for them, and re-layouts  17.7 us (5%)
  starting transfers between devices  16.7 us (5%)
  between operations  13.6 us (4%)
    all_to_all x1, waiting for transfers between devices, body(): lax.all_to_all(sending.reshape((shards, MOST) + database.shape[1:]), 'seq...  92.7 us
    psum x1, waiting for transfers between devices, body(): lax.psum(jnp.dot(hidden_act, w_out, preferred_element_type=jnp.float32).a...  81.8 us
    all_gather x1, waiting for transfers between devices, body(): blocks = lax.all_gather(blocks, 'mp', axis=4, tiled=True)  47.7 us
    all_to_all x1, starting transfers between devices, body(): lax.all_to_all(sending.reshape((shards, MOST) + database.shape[1:]), 'seq...  12 us
    dot_general x1, matrix products, body(): jnp.dot(hidden_act, w_out, preferred_element_type=jnp.float32)  10.9 us
    dot_general x1, matrix products, body(): jnp.einsum('schqk,sckhd->scqhd', weights, value_rows, preferred_element_t...  10.3 us
    unnamed x19, local copies, waits for them, and re-layouts  7.25 us
    reduce_sum x2, other arithmetic, rms_scale(): jnp.mean(values * values, axis=-1, keepdims=True) + epsilon  6.65 us
  transfers between devices with their start and end apart: 4, of which 4 were waited for; matrix products, arithmetic and copies ran while one was open for 0% of the time, Pallas kernels for 0%

commit v1 on v0

--- a/solution.py
+++ b/solution.py
@@ -6,6 +6,28 @@
 HD = 128
 MOST = 2
 epsilon = 1e-06
+
+
+def joined_along(blocks, dim):
+    lengths = list(blocks.shape[1:])
+    lengths[dim] *= blocks.shape[0]
+    return jnp.moveaxis(blocks, 0, dim).reshape(lengths)
+
+
+def collected_by_bits(array, axis):
+    size = lax.axis_size(axis)
+    blocks = array[None]
+    for level in range(size.bit_length() - 1):
+        stride = 1 << level
+        other = lax.ppermute(blocks, axis, [(i, i ^ stride) for i in range(size)])
+        both = jnp.stack([blocks, other])
+        upper = lax.axis_index(axis) >> level & 1
+        blocks = jnp.where(upper == 0, both, both[::-1]).reshape(-1, *array.shape)
+    return blocks
+
+
+def doubled_up(value, axis, dim):
+    return joined_along(collected_by_bits(value, axis), dim)
 
 
 def passed_along(array, axis, by):
@@ -55,7 +77,7 @@
     blocks = blocks.reshape((seq_count, per_span, neigh_count, block_len, blocks.shape[-1]))
     arrived_rows = passed_along(blocks[:, -1], "seq", 1)
     blocks = jnp.concatenate([arrived_rows[:, None], blocks[:, :-1]], axis=1)
-    blocks = lax.all_gather(blocks, "mp", axis=4, tiled=True)
+    blocks = doubled_up(blocks, "mp", 4)
     features = blocks.shape[-1]
     widened = blocks.reshape(-1, features).astype(jnp.float32)
     normed = rms_scale(widened, pre_gain).astype(jnp.bfloat16)

time: 325 us -> 348 us (1.071)
  local copies, waits for them, and re-layouts: 17.7 us -> 27.8 us
  waiting for transfers between devices: 227 us -> 232 us
  starting transfers between devices: 16.7 us -> 20.9 us
  other arithmetic: 19.3 us -> 23 us
    all_gather x1 -> x0, waiting for transfers between devices: 47.7 us -> none  [body(): blocks = lax.all_gather(blocks, 'mp', axis=4, tiled=True)]
    ppermute x0 -> x2, waiting for transfers between devices: none -> 45.1 us  [collected_by_bits(): other = lax.ppermute(blocks, axis, [(i, i ^ stride) for i in range(size)])]
    psum x1, waiting for transfers between devices: 81.8 us -> 88.7 us  [body(): lax.psum(jnp.dot(hidden_act, w_out, preferred_element_type=jnp.float32).a...]
    convert_element_type x0 -> x1, local copies, waits for them, and re-layouts: none -> 6.85 us  [body(): widened = blocks.reshape(-1, features).astype(jnp.float32)]
    ppermute x0 -> x2, starting transfers between devices: none -> 4.3 us  [collected_by_bits(): other = lax.ppermute(blocks, axis, [(i, i ^ stride) for i in range(size)])]
    another operation x0 -> x4, other arithmetic: none -> 3.62 us  [collected_by_bits(): both = jnp.stack([blocks, other])]
    unnamed x19 -> x22, local copies, waits for them, and re-layouts: 7.25 us -> 10.5 us
  transfers between devices with their start and end apart: 4 -> 5, of which waited for: 4 -> 5; matrix products, arithmetic and copies ran while one was open for 0% -> 0% of each run, Pallas kernels for 0% -> 0%
where the time goes in v1:
time: 348 us
  waiting for transfers between devices  232 us (67%)
  matrix products  30.7 us (9%)
  local copies, waits for them, and re-layouts  27.8 us (8%)
  other arithmetic  23 us (7%)
  starting transfers between devices  20.9 us (6%)
  between operations  13.7 us (4%)
    all_to_all x1, waiting for transfers between devices, body(): lax.all_to_all(sending.reshape((shards, MOST) + database.shape[1:]), 'seq...  92.7 us
    psum x1, waiting for transfers between devices, body(): lax.psum(jnp.dot(hidden_act, w_out, preferred_element_type=jnp.float32).a...  88.7 us
    ppermute x2, waiting for transfers between devices, collected_by_bits(): other = lax.ppermute(blocks, axis, [(i, i ^ stride) for i in range(size)])  45.1 us
    all_to_all x1, starting transfers between devices, body(): lax.all_to_all(sending.reshape((shards, MOST) + database.shape[1:]), 'seq...  12 us
    dot_general x1, matrix products, body(): jnp.dot(hidden_act, w_out, preferred_element_type=jnp.float32)  11.6 us
    unnamed x22, local copies, waits for them, and re-layouts  10.5 us
    dot_general x1, matrix products, body(): jnp.einsum('schqk,sckhd->scqhd', weights, value_rows, preferred_element_t...  10.4 us
  transfers between devices with their start and end apart: 5, of which 5 were waited for; matrix products, arithmetic and copies ran while one was open for 0% of the time, Pallas kernels for 0%

profile of v1, /device:TPU:1, one launch (start us, length us, event | category | flops | bytes accessed | tf_op | source)
XLA Modules:
  0.0 347.8 jit_solution(7676948731739661471)
XLA Ops:
  6.5 0.8 reshape_squeeze.3
  8.6 2.8 gather_fusion
  11.4 4.5 %broadcast_select_fusion = bf16[32,2,128,256]{3,2,1,0:T(8,128)(2,1)} fusion(bf16[32,2,128,256]{3,2,1,0:T(8,128)(2,1)} %bitcast.81, pred[32,2]{1,0:T(8,128)(4,1)S(1)} %copy.41), kind=kLoop, calls=%fused_computation.18 | loop fusion | flops 2097152 | bytes 8388672 | tf_op jit(solution)/shard_map/jit(_take)/select_n | solution.py:67
  15.9 12.0 %all-to-all-start = ((bf16[32,2,128,256]{3,2,1,0:T(8,128)(2,1)}), bf16[32,2,128,256]{3,2,1,0:T(8,128)(2,1)}, u32[]{:S(2)}, u32[]{:S(2)}) async-start(bf16[32,2,128,256]{3,2,1,0:T(8,128)(2,1)} %broadcast_select_fusion), calls=%async_computation | async-start | bytes 8388608 | tf_op jit(solution)/shard_map/all_to_all | solution.py:68
  28.3 92.7 %all-to-all-done = bf16[32,2,128,256]{3,2,1,0:T(8,128)(2,1)} async-done(((bf16[32,2,128,256]{3,2,1,0:T(8,128)(2,1)}), bf16[32,2,128,256]{3,2,1,0:T(8,128)(2,1)}, u32[]{:S(2)}, u32[]{:S(2)}) %all-to-all-start) | async-done | bytes 4194336 | tf_op jit(solution)/shard_map/all_to_all | solution.py:68
  121.0 2.8 gather_fusion.1
  124.0 4.6 %collective-permute-start = (bf16[3,2,128,256]{3,2,1,0:T(8,128)(2,1)S(1)}, bf16[3,2,128,256]{3,2,1,0:T(8,128)(2,1)S(1)}, u32[]{:S(2)}, u32[]{:S(2)}) collective-permute-start(bf16[3,2,128,256]{3,2,1,0:T(8,128)(2,1)S(1)} %get-tuple-element.9), channel_id=1, source_target_pairs={{0,4},{4,8},{8,12},{12,16},{16,20},{20,24},{24,28},{28,32},{32,36}... | collective-permute-start | bytes 1179656 | tf_op jit(solution)/shard_map/ppermute | solution.py:36
  128.6 5.2 %collective-permute-done = bf16[3,2,128,256]{3,2,1,0:T(8,128)(2,1)S(1)} collective-permute-done((bf16[3,2,128,256]{3,2,1,0:T(8,128)(2,1)S(1)}, bf16[3,2,128,256]{3,2,1,0:T(8,128)(2,1)S(1)}, u32[]{:S(2)}, u32[]{:S(2)}) %collective-permute-start) | collective-permute-done | bytes 393248 | tf_op jit(solution)/shard_map/ppermute | solution.py:36
  133.9 1.4 collective-permute-start.1
  135.2 13.7 %collective-permute-done.1 = bf16[1,3,2,2,128,256]{5,4,3,2,1,0:T(8,128)(2,1)S(1)} collective-permute-done((bf16[1,3,2,2,128,256]{5,4,3,2,1,0:T(8,128)(2,1)S(1)}, bf16[1,3,2,2,128,256]{5,4,3,2,1,0:T(8,128)(2,1)S(1)}, u32[]{:S(2)}, u32[]{:S(2)}) %collective-permute-start.1) | collective-permute-done | bytes 786464 | tf_op jit(solution)/shard_map/ppermute | solution.py:22
  149.1 1.7 fusion.32
  150.8 2.9 collective-permute-start.2
  153.7 31.4 %collective-permute-done.2 = bf16[2,3,2,2,128,256]{5,4,3,2,1,0:T(8,128)(2,1)} collective-permute-done((bf16[2,3,2,2,128,256]{5,4,3,2,1,0:T(8,128)(2,1)}, bf16[2,3,2,2,128,256]{5,4,3,2,1,0:T(8,128)(2,1)}, u32[]{:S(2)}, u32[]{:S(2)}) %collective-permute-start.2) | collective-permute-done | bytes 1572896 | tf_op jit(solution)/shard_map/ppermute | solution.py:22
  185.1 1.7 pad_maximum_fusion
  186.8 0.9 multiply_reduce_fusion.1
  187.7 3.5 fusion.9
  191.2 6.9 %copy.44 = f32[4,3,2,2,128,256]{5,0,4,3,2,1:T(4,128)S(1)} copy(f32[4,3,2,2,128,256]{5,4,3,2,1,0:T(8,128)} %bitcast.79) | data formatting | bytes 12582912 | tf_op jit(solution)/shard_map/convert_element_type | solution.py:82
  198.1 4.2 %copy.49 = f32[192,8,4,256]{3,1,2,0:T(8,128)} copy(f32[192,8,4,256]{3,2,1,0:T(4,128)S(1)} %bitcast.80) | data formatting | bytes 12582912
  202.3 11.6 %convolution_convert_fusion.2 = bf16[1536,1024]{1,0:T(8,128)(2,1)} fusion(bf16[1024,1024]{1,0:T(8,128)(2,1)} %param.17, bf16[1024,1024]{1,0:T(8,128)(2,1)} %param.16, f32[1536,1024]{1,0:T(8,128)} %bitcast.76, f32[1024]{0:T(1024)S(1)} %copy-done.8, f32[1536]{0:T(1024)S(1)} %rsqrt.20), kind=kOutput, calls=%fused_computation.21 | convolution fusion | flops 6462898176 | bytes 13641728 | tf_op jit(solution)/shard_map/dot_general | solution.py:88
  213.9 1.1 copy-done.4
  215.2 88.7 %all-reduce.2.cloned.1.call-done = bf16[1536,1024]{1,0:T(8,128)(2,1)} async-done(((bf16[1536,1024]{1,0:T(8,128)(2,1)}), bf16[1536,1024]{1,0:T(8,128)(2,1)}) %all-reduce.2.cloned.1.call-update) | async-done | bytes 3145744 | tf_op jit(solution)/shard_map/psum | solution.py:87
  303.9 4.7 %multiply_reduce_fusion = f32[1536]{0:T(1024)S(1)} fusion(f32[1536,1024]{1,0:T(8,128)} %bitcast.77, bf16[1536,1024]{1,0:T(8,128)(2,1)} %all-reduce.2.cloned.1.call-done), kind=kLoop, calls=%fused_computation.13 | loop fusion | flops 6289920 | bytes 9443328 | tf_op jit(solution)/shard_map/reduce_sum | solution.py:42
  308.7 4.1 %multiply_convert_fusion = bf16[1536,1024]{1,0:T(8,128)(2,1)S(1)} fusion(f32[1536,1024]{1,0:T(8,128)} %bitcast.78, bf16[1536,1024]{1,0:T(8,128)(2,1)S(1)} %copy-done.2, f32[1024]{0:T(1024)S(1)} %copy-done.5, f32[1536]{0:T(1024)S(1)} %add_rsqrt_fusion), kind=kLoop, calls=%fused_computation.12 | loop fusion | flops 7864320 | bytes 12593152 | tf_op jit(solution)/shard_map/convert_element_type | solution.py:90
  312.8 3.6 %fusion.23 = bf16[192,8,8,128]{3,1,2,0:T(8,128)(2,1)S(1)} fusion(bf16[1536,1024]{1,0:T(8,128)(2,1)S(1)} %multiply_convert_fusion, bf16[1024,1024]{1,0:T(8,128)(2,1)S(1)} %copy-done.6), kind=kOutput, calls=%fused_computation.39 | convolution fusion | flops 3222798336 | bytes 8388608 | tf_op jit(solution)/shard_map/dot_general | solution.py:91
  316.4 3.9 %fusion.22 = bf16[192,8,8,128]{3,1,2,0:T(8,128)(2,1)S(1)} fusion(bf16[1536,1024]{1,0:T(8,128)(2,1)S(1)} %multiply_convert_fusion, bf16[1024,1024]{1,0:T(8,128)(2,1)S(1)} %copy-done.7), kind=kOutput, calls=%fused_computation.38 | convolution fusion | flops 3222798336 | bytes 8388608 | tf_op jit(solution)/shard_map/dot_general | solution.py:92
  320.3 2.5 copy.53
  323.6 1.2 fusion.15
  324.8 1.7 copy-done.3
  326.5 1.1 fusion.51
  327.7 10.4 %fusion.28 = bf16[3,2,64,8,128]{4,2,3,1,0:T(8,128)(2,1)} fusion(bf16[3,2,256,8,128]{4,3,2,1,0:T(8,128)(2,1)} %bitcast.84, f32[3,2,8,64]{3,2,1,0:T(8,128)S(1)} %fusion.51, pred[2]{0:T(512)(128)(4,1)S(1)} %add_compare_fusion, f32[3,2,8,256,64]{3,4,2,1,0:T(8,128)} %copy-done.3), kind=kOutput, calls=%fused_computation.44 | convolution fusion | flops 206048512 | bytes 7090178 | tf_op jit(solution)/shard_map/schqk,sckhd->scqhd/dot_general | solution.py:106
  338.1 1.7 copy.48
  339.8 1.2 reshape.166
  (44 shorter events, 3.0 us)
Async XLA Ops:
  6.5 2.0 copy-start
  15.9 105.0 %all-to-all-start = ((bf16[32,2,128,256]{3,2,1,0:T(8,128)(2,1)}), bf16[32,2,128,256]{3,2,1,0:T(8,128)(2,1)}, u32[]{:S(2)}, u32[]{:S(2)}) async-start(bf16[32,2,128,256]{3,2,1,0:T(8,128)(2,1)} %broadcast_select_fusion), calls=%async_computation | async-start | bytes 8388608 | tf_op jit(solution)/shard_map/all_to_all | solution.py:68
  27.9 276.0 %all-reduce.2.cloned.1.call-start = ((), (), s32[]{:S(2)}) async-start(), calls=%async_computation.1 | async-start | bytes 6291456 | tf_op jit(solution)/shard_map/psum | solution.py:87
  124.0 9.8 %collective-permute-start = (bf16[3,2,128,256]{3,2,1,0:T(8,128)(2,1)S(1)}, bf16[3,2,128,256]{3,2,1,0:T(8,128)(2,1)S(1)}, u32[]{:S(2)}, u32[]{:S(2)}) collective-permute-start(bf16[3,2,128,256]{3,2,1,0:T(8,128)(2,1)S(1)} %get-tuple-element.9), channel_id=1, source_target_pairs={{0,4},{4,8},{8,12},{12,16},{16,20},{20,24},{24,28},{28,32},{32,36}... | collective-permute-start | bytes 1179656 | tf_op jit(solution)/shard_map/ppermute | solution.py:36
  133.9 15.1 %collective-permute-start.1 = (bf16[1,3,2,2,128,256]{5,4,3,2,1,0:T(8,128)(2,1)S(1)}, bf16[1,3,2,2,128,256]{5,4,3,2,1,0:T(8,128)(2,1)S(1)}, u32[]{:S(2)}, u32[]{:S(2)}) collective-permute-start(bf16[1,3,2,2,128,256]{5,4,3,2,1,0:T(8,128)(2,1)S(1)} %get-tuple-element.8), channel_id=1, source_target_pairs={{0,1},{1,0},{2,3},{3,2},{4,5},{5,4},{6,7},{7,6},{8,9},{9,8},{10,11... | collective-permute-start | bytes 2359304 | tf_op jit(solution)/shard_map/ppermute | solution.py:22
  150.8 34.3 %collective-permute-start.2 = (bf16[2,3,2,2,128,256]{5,4,3,2,1,0:T(8,128)(2,1)}, bf16[2,3,2,2,128,256]{5,4,3,2,1,0:T(8,128)(2,1)}, u32[]{:S(2)}, u32[]{:S(2)}) collective-permute-start(bf16[2,3,2,2,128,256]{5,4,3,2,1,0:T(8,128)(2,1)} %get-tuple-element.6), channel_id=1, source_target_pairs={{0,2},{1,3},{2,0},{3,1},{4,6},{5,7},{6,4},{7,5},{8,10},{9,11},{10,... | collective-permute-start | bytes 4718600 | tf_op jit(solution)/shard_map/ppermute | solution.py:22
  198.1 4.2 %copy-start.8 = (f32[1024]{0:T(1024)S(1)}, f32[1024]{0:T(1024)}, u32[]{:S(2)}) copy-start(f32[1024]{0:T(1024)} %param.14) | copy-start | bytes 12292
  213.8 1.1 copy-start.4
  215.2 93.5 %copy-start.5 = (f32[1024]{0:T(1024)S(1)}, f32[1024]{0:T(1024)}, u32[]{:S(2)}) copy-start(f32[1024]{0:T(1024)} %param.15) | copy-start | bytes 12292
  303.9 4.8 %copy-start.2 = (bf16[1536,1024]{1,0:T(8,128)(2,1)S(1)}, bf16[1536,1024]{1,0:T(8,128)(2,1)}, u32[]{:S(2)}) copy-start(bf16[1536,1024]{1,0:T(8,128)(2,1)} %all-reduce.2.cloned.1.call-done) | copy-start | bytes 9437188
  308.7 4.1 %copy-start.6 = (bf16[1024,1024]{1,0:T(8,128)(2,1)S(1)}, bf16[1024,1024]{1,0:T(8,128)(2,1)}, u32[]{:S(2)}) copy-start(bf16[1024,1024]{1,0:T(8,128)(2,1)} %param.18) | copy-start | bytes 6291460
  312.8 3.6 %copy-start.7 = (bf16[1024,1024]{1,0:T(8,128)(2,1)S(1)}, bf16[1024,1024]{1,0:T(8,128)(2,1)}, u32[]{:S(2)}) copy-start(bf16[1024,1024]{1,0:T(8,128)(2,1)} %param.19) | copy-start | bytes 6291460
  324.8 1.7 copy-start.3
  327.7 13.3 %copy-start.1 = (bf16[32,128,256]{2,1,0:T(8,128)(2,1)S(1)}, bf16[32,128,256]{2,1,0:T(8,128)(2,1)}, u32[]{:S(2)}) copy-start(bf16[32,128,256]{2,1,0:T(8,128)(2,1)} %param.11) | copy-start | bytes 6291460
Sparse Core Ops, SparseCore 0:
  214.0 89.8 all-reduce.1
